TPU v7x, 32 devices: a whole 2x2x4 slice. The times are simulated.
32 devices in a mesh: seq: 8 (over z, y), rep: 4 (over x, core).
Axes of the slice: x: 2, y: 2, z: 4, core: 2. Of those that a mesh axis runs over, the one named last changes fastest.
Arguments:
- queries: bfloat16 [32, 32, 128], P('seq', 'rep'), may hold values from -48 to 48
- key_cache: bfloat16 [8, 16384, 128], P('rep', 'seq'), may hold values from -6 to 6
- value_cache: bfloat16 [8, 16384, 128], P('rep', 'seq'), may hold values from -6 to 6
- summary_keys: bfloat16 [8, 8, 128], P('rep', 'seq'), may hold values from -16 to 16
- summary_values: bfloat16 [8, 8, 128], P('rep', 'seq'), may hold values from -6 to 6
- owner_map: int32 [8], replicated, may hold values from 0 to 7, each once
- super_ids: int32 [32, 8, 4], P(None, 'rep'), may hold values from 0 to 7, as said below
- fine_ids: int32 [32, 8, 16], P(None, 'rep'), may hold values from 0 to 63, all different within a row
Outputs:
- attended: bfloat16 [32, 32, 128], P(('seq', 'rep'))
Inputs may be any that keep to these rules, and one draw needn't show every extreme that they name: `super_ids`: each row names 4 different super-blocks; among the rows of one sender group (the 4 requests of one index of seq with the 2 key-value heads of one index of rep) no super-block is named more than 5 times, and in every such group some super-block is named exactly 5 times. `fine_ids`: each row names 16 different positions; position p is block p % 16 of super-block super_ids[r, g, p // 16]. `owner_map`: a permutation; slot q covers fine blocks q * 16 to q * 16 + 15 of the caches.
All inputs are finite; a program needn't handle non-finite values.
Results may differ from a plain program's by a relative error of at most 0.004.
Values may be sent and summed in bfloat16 or wider, within the bound.
A program may use at most 64 MiB of HBM per device.

v0:
```python
import math

import jax
import jax.numpy as jnp
from jax import lax
from jax.sharding import PartitionSpec as P

BLK = 128
SUPER = 16


NEGATIVE = -1e30


def combine(earlier, later):
    highest = jnp.maximum(earlier[0], later[0])
    left_factor = jnp.exp(earlier[0] - highest)
    right_factor = jnp.exp(later[0] - highest)
    return (
        highest,
        earlier[1] * left_factor + later[1] * right_factor,
        earlier[2] * left_factor[..., None] + later[2] * right_factor[..., None],
    )


def coarse_terms(query_rows, summary_keys, summary_values, kept_slots):
    scaling = query_rows.shape[-1] ** (-0.5)
    scores = jnp.einsum(
        "bgqd,gsd->bgqs", query_rows, summary_keys, preferred_element_type=jnp.float32
    ) * scaling + math.log(SUPER)
    scores = jnp.where(kept_slots[:, :, None, :], scores, NEGATIVE)
    highest = jnp.max(scores, axis=3)
    weights = jnp.where(kept_slots[:, :, None, :], jnp.exp(scores - highest[..., None]), 0.0)
    weighted = jnp.einsum("bgqs,gsd->bgqd", weights, summary_values.astype(jnp.float32))
    return (highest, jnp.sum(weights, axis=3), weighted)


def fine_terms(query_rows, key_cache, value_cache, block_mask):
    scaling = query_rows.shape[-1] ** (-0.5)
    scores = (
        jnp.einsum("bgqd,gtd->bgqt", query_rows, key_cache, preferred_element_type=jnp.float32)
        * scaling
    )
    row_count, groups, per_group, tokens = scores.shape
    block_count = block_mask.shape[2]
    shaped = scores.reshape(row_count, groups, per_group, block_count, tokens // block_count)
    token_mask = block_mask[:, :, None, :, None]
    shaped = jnp.where(token_mask, shaped, NEGATIVE)
    highest = jnp.max(shaped, axis=(3, 4))
    weights = jnp.where(token_mask, jnp.exp(shaped - highest[..., None, None]), 0.0)
    weight_sum = jnp.sum(weights, axis=(3, 4))
    weighted = jnp.einsum(
        "bgqt,gtd->bgqd",
        weights.reshape(row_count, groups, per_group, tokens),
        value_cache.astype(jnp.float32),
    )
    return (highest, weight_sum, weighted)


def shards(
    queries, key_cache, value_cache, summary_keys, summary_values, owner_map, super_ids, fine_ids
):
    groups = key_cache.shape[0]
    head_dim = queries.shape[2]
    per_group = queries.shape[1] // groups
    blocks_here = key_cache.shape[1] // BLK
    supers_here = summary_keys.shape[1]
    slot_count = owner_map.shape[0]
    chosen_count = super_ids.shape[2]
    my_index = lax.axis_index("seq")
    seq_size = lax.axis_size("seq")
    own_rows = queries.shape[0]
    is_super = super_ids[..., None] == jnp.arange(slot_count, dtype=jnp.int32)
    slots = jnp.sum(jnp.where(is_super, owner_map, 0), axis=3)
    everyone = lax.all_gather(queries, "seq", axis=0, tiled=True)
    requests = everyone.shape[0]
    is_chosen = (fine_ids // SUPER)[..., None] == jnp.arange(chosen_count, dtype=jnp.int32)
    picked = jnp.sum(jnp.where(is_chosen, slots[:, :, None, :], 0), axis=3)
    chosen = picked * SUPER + fine_ids % SUPER
    local_blocks = my_index * blocks_here + jnp.arange(blocks_here, dtype=jnp.int32)
    block_mask = jnp.any(chosen[..., None] == local_blocks, axis=2)
    local_slots = my_index * supers_here + jnp.arange(supers_here, dtype=jnp.int32)
    kept_local = jnp.logical_not(jnp.any(slots[..., None] == local_slots, axis=2))
    row_step = math.gcd(requests, 64)
    grouped = everyone.reshape(requests // row_step, row_step, groups, per_group, head_dim)
    masks = block_mask.reshape(requests // row_step, row_step, groups, blocks_here)
    kept_blocks = kept_local.reshape(requests // row_step, row_step, groups, supers_here)

    def owner_step(pieces):
        fine_part = fine_terms(pieces[0], key_cache, value_cache, pieces[1])
        return combine(fine_part, coarse_terms(pieces[0], summary_keys, summary_values, pieces[2]))

    highest, weight_sum, weighted = lax.map(owner_step, (grouped, masks, kept_blocks))
    highest = highest.reshape(requests, groups, per_group)
    weight_sum = weight_sum.reshape(requests, groups, per_group)
    weighted = weighted.reshape(requests, groups, per_group, head_dim)
    peak_all, sum_all, weighted_all = (
        lax.all_to_all(highest, "seq", split_axis=0, concat_axis=0, tiled=True),
        lax.all_to_all(weight_sum, "seq", split_axis=0, concat_axis=0, tiled=True),
        lax.all_to_all(weighted, "seq", split_axis=0, concat_axis=0, tiled=True),
    )
    peak_all = peak_all.reshape(seq_size, own_rows, groups, per_group)
    sum_all = sum_all.reshape(seq_size, own_rows, groups, per_group)
    weighted_all = weighted_all.reshape(seq_size, own_rows, groups, per_group, head_dim)
    global_peak = jnp.max(peak_all, axis=0)
    factor = jnp.exp(peak_all - global_peak)
    merged = (
        global_peak,
        jnp.sum(sum_all * factor, axis=0),
        jnp.sum(weighted_all * factor[..., None], axis=0),
    )
    result = (
        (merged[2] / merged[1][..., None])
        .reshape(own_rows, groups * per_group, head_dim)
        .astype(jnp.bfloat16)
    )
    return lax.all_to_all(result, "rep", split_axis=0, concat_axis=1, tiled=True)


def solution(mesh):
    in_specs = (
        P("seq", "rep", None),
        P("rep", "seq", None),
        P("rep", "seq", None),
        P("rep", "seq", None),
        P("rep", "seq", None),
        P(),
        P(None, "rep", None),
        P(None, "rep", None),
    )
    out_specs = P(("seq", "rep"), None, None)
    return jax.shard_map(shards, mesh=mesh, in_specs=in_specs, out_specs=out_specs, check_vma=False)
```

profile of v0, /device:TPU:0, one launch (start us, length us, event | category | flops | bytes accessed | tf_op | source)
XLA Modules:
  0.0 78.4 jit_solution(1000240382717264927)
XLA Ops:
  0.0 0.0 copy-start
  0.0 0.9 %select_reduce_fusion.1 = s32[32,2,4]{0,2,1:T(4,128)S(1)} fusion(s32[8]{0:T(128)} %param.13, s32[32,2,4]{0,2,1:T(4,128)} %param.14), kind=kLoop, calls=%fused_computation.22 | loop fusion | flops 5888 | bytes 2080 | tf_op jit(solution)/shard_map/reduce_sum | solution.py:74
  0.9 0.7 add_select_fusion.1
  1.7 0.7 fusion.13
  2.4 0.1 compare_reduce_fusion
  2.5 0.1 copy.44
  2.6 32.6 %all_gather.3 = bf16[32,8,128]{2,1,0:T(8,128)(2,1)S(1)} all-gather(bf16[4,8,128]{2,1,0:T(8,128)(2,1)} %param.8), channel_id=1, replica_groups=mesh['seq'=8,'rep'=4] {'seq'}, dimensions={0}, use_global_device_ids=true | all-gather | bytes 73728 | tf_op jit(solution)/shard_map/all_gather | solution.py:75
  35.2 0.2 broadcast_in_dim.107
  35.4 0.1 broadcast_in_dim.108
  35.6 0.8 %fusion.25 = f32[2,1,32,4]{2,1,3,0:T(1,128)S(1)} fusion(bf16[32,2,4,128]{3,0,2,1:T(8,128)(2,1)S(1)} %bitcast.85, bf16[2,128,1,1]{1,0,2,3:T(2,128)(2,1)} %bitcast.96), kind=kOutput, calls=%fused_computation.50 | convolution fusion | flops 65536 | bytes 67072 | tf_op jit(solution)/shard_map/while/body/eval_jaxpr/bgqd,gsd->bgqs/dot_general | solution.py:28
  36.4 0.0 copy-done
  36.4 0.6 fusion.28
  37.0 0.6 fusion.2
  37.6 0.7 copy.47
  38.3 5.5 %all-to-all-start.1 = ((f32[32,2,4]{2,1,0:T(2,128)}), f32[32,2,4]{2,1,0:T(2,128)S(1)}, u32[]{:S(2)}, u32[]{:S(2)}) async-start(f32[32,2,4]{2,1,0:T(2,128)} %copy.47), calls=%async_computation.1 | async-start | bytes 65536 | tf_op jit(solution)/shard_map/all_to_all | solution.py:98
  43.8 0.0 copy-done.1
  43.8 0.7 copy.50
  44.5 6.0 %all-to-all-done.1 = f32[32,2,4]{2,1,0:T(2,128)S(1)} async-done(((f32[32,2,4]{2,1,0:T(2,128)}), f32[32,2,4]{2,1,0:T(2,128)S(1)}, u32[]{:S(2)}, u32[]{:S(2)}) %all-to-all-start.1) | async-done | bytes 1056 | tf_op jit(solution)/shard_map/all_to_all | solution.py:98
  50.4 3.3 %all-to-all-start.2 = ((f32[32,2,4]{2,1,0:T(2,128)}), f32[32,2,4]{2,1,0:T(2,128)S(1)}, u32[]{:S(2)}, u32[]{:S(2)}) async-start(f32[32,2,4]{2,1,0:T(2,128)} %copy.50), calls=%async_computation.2 | async-start | bytes 65536 | tf_op jit(solution)/shard_map/all_to_all | solution.py:99
  53.8 1.8 %fusion.6 = f32[32,2,4,128]{3,0,2,1:T(8,128)S(1)} fusion(f32[32,2,4,2048]{3,0,2,1:T(8,128)S(1)} %get-tuple-element.44, bf16[2,2048,128]{2,1,0:T(8,128)(2,1)} %param.10, f32[32,2,4]{0,2,1:T(4,128)S(1)} %get-tuple-element.32, pred[32,2,2048]{2,0,1:T(8,128)(4,1)S(1)} %broadcast_in_dim.108, f32[32,2,4]{0,2,1:T(4,128)S(1)} %get-tuple-element.30, ...), kind=kOutput, calls=%fused_computation.8 | convolution fusion | flops 135397376 | bytes 3412992 | tf_op jit(solution)/shard_map/while/body/eval_jaxpr/bgqt,gtd->bgqd/dot_general | solution.py:52
  55.6 0.7 copy.46
  56.3 4.3 %all-to-all-done.2 = f32[32,2,4]{2,1,0:T(2,128)S(1)} async-done(((f32[32,2,4]{2,1,0:T(2,128)}), f32[32,2,4]{2,1,0:T(2,128)S(1)}, u32[]{:S(2)}, u32[]{:S(2)}) %all-to-all-start.2) | async-done | bytes 1056 | tf_op jit(solution)/shard_map/all_to_all | solution.py:99
  60.6 3.4 %all-to-all-start = ((f32[32,2,4,128]{3,2,1,0:T(4,128)}), f32[32,2,4,128]{3,2,1,0:T(4,128)S(1)}, u32[]{:S(2)}, u32[]{:S(2)}) async-start(f32[32,2,4,128]{3,2,1,0:T(4,128)} %copy.46), calls=%async_computation | async-start | bytes 262144 | tf_op jit(solution)/shard_map/all_to_all | solution.py:100
  64.0 0.2 copy.58
  64.2 0.1 copy.61
  64.3 0.2 copy.59
  64.5 0.1 copy.60
  64.6 6.6 %all-to-all-done = f32[32,2,4,128]{3,2,1,0:T(4,128)S(1)} async-done(((f32[32,2,4,128]{3,2,1,0:T(4,128)}), f32[32,2,4,128]{3,2,1,0:T(4,128)S(1)}, u32[]{:S(2)}, u32[]{:S(2)}) %all-to-all-start) | async-done | bytes 131104 | tf_op jit(solution)/shard_map/all_to_all | solution.py:100
  71.3 0.1 fusion.12
  71.4 0.1 fusion.14
  71.5 6.4 %all_to_all.27 = bf16[4,8,128]{2,1,0:T(8,128)(2,1)S(1)} all-to-all(bf16[4,8,128]{2,1,0:T(8,128)(2,1)S(1)} %fusion.14), channel_id=1, replica_groups=mesh['seq'=8,'rep'=4] {'rep'}, dimensions={0} | all-to-all | bytes 16384 | tf_op jit(solution)/shard_map/all_to_all | solution.py:117
  77.8 0.6 copy.71
  (11 shorter events, 0.2 us)
Async XLA Ops:
  0.0 36.4 %copy-start = (bf16[2,2048,128]{2,1,0:T(8,128)(2,1)S(1)}, bf16[2,2048,128]{2,1,0:T(8,128)(2,1)}, u32[]{:S(2)}) copy-start(bf16[2,2048,128]{2,1,0:T(8,128)(2,1)} %param.9) | copy-start | bytes 3145732
  36.4 7.4 %copy-start.1 = (bf16[2,1,128]{2,0,1:T(2,128)(2,1)S(1)}, bf16[2,1,128]{2,0,1:T(2,128)(2,1)}, u32[]{:S(2)}) copy-start(bf16[2,1,128]{2,0,1:T(2,128)(2,1)} %param.12) | copy-start | bytes 1540
  38.3 12.2 %all-to-all-start.1 = ((f32[32,2,4]{2,1,0:T(2,128)}), f32[32,2,4]{2,1,0:T(2,128)S(1)}, u32[]{:S(2)}, u32[]{:S(2)}) async-start(f32[32,2,4]{2,1,0:T(2,128)} %copy.47), calls=%async_computation.1 | async-start | bytes 65536 | tf_op jit(solution)/shard_map/all_to_all | solution.py:98
  50.4 10.2 %all-to-all-start.2 = ((f32[32,2,4]{2,1,0:T(2,128)}), f32[32,2,4]{2,1,0:T(2,128)S(1)}, u32[]{:S(2)}, u32[]{:S(2)}) async-start(f32[32,2,4]{2,1,0:T(2,128)} %copy.50), calls=%async_computation.2 | async-start | bytes 65536 | tf_op jit(solution)/shard_map/all_to_all | solution.py:99
  60.6 10.7 %all-to-all-start = ((f32[32,2,4,128]{3,2,1,0:T(4,128)}), f32[32,2,4,128]{3,2,1,0:T(4,128)S(1)}, u32[]{:S(2)}, u32[]{:S(2)}) async-start(f32[32,2,4,128]{3,2,1,0:T(4,128)} %copy.46), calls=%async_computation | async-start | bytes 262144 | tf_op jit(solution)/shard_map/all_to_all | solution.py:100
where the time goes:
time: 79.1 us; the launch traced here: 78.4 us
  blocking collectives  38.9 us (49%)
  waiting for transfers between devices  16.9 us (21%)
  starting transfers between devices  12.2 us (15%)
  local copies, waits for them, and re-layouts  3.75 us (5%)
  other arithmetic  3.39 us (4%)
  matrix products  3.23 us (4%)
    all_gather x1, blocking collectives, shards(): everyone = lax.all_gather(queries, 'seq', axis=0, tiled=True)  32.6 us
    all_to_all x1, waiting for transfers between devices, shards(): lax.all_to_all(weighted, 'seq', split_axis=0, concat_axis=0, tiled=True)  6.62 us
    all_to_all x1, blocking collectives, shards(): lax.all_to_all(result, 'rep', split_axis=0, concat_axis=1, tiled=True)  6.37 us
    all_to_all x1, waiting for transfers between devices, shards(): lax.all_to_all(highest, 'seq', split_axis=0, concat_axis=0, tiled=True)  5.95 us
    all_to_all x1, starting transfers between devices, shards(): lax.all_to_all(highest, 'seq', split_axis=0, concat_axis=0, tiled=True)  5.49 us
    all_to_all x1, waiting for transfers between devices, shards(): lax.all_to_all(weight_sum, 'seq', split_axis=0, concat_axis=0, tiled=True)  4.27 us
    all_to_all x1, starting transfers between devices, shards(): lax.all_to_all(weighted, 'seq', split_axis=0, concat_axis=0, tiled=True)  3.37 us
    all_to_all x1, starting transfers between devices, shards(): lax.all_to_all(weight_sum, 'seq', split_axis=0, concat_axis=0, tiled=True)  3.32 us
  transfers between devices with their start and end apart: 3, of which 3 were waited for; matrix products, arithmetic and copies ran while one was open for 5% of the time, Pallas kernels for 0%

commit v1 on v0

v1 whole, which is shorter than its diff:
```python
import functools
import math

import jax
import jax.numpy as jnp
from jax import lax
from jax.experimental import pallas as pl
from jax.experimental.pallas import tpu as pltpu
from jax.sharding import PartitionSpec as P

BLK = 128
SUPER = 16
NEGATIVE = -1e30
LOG2E = math.log2(math.e)
CHUNK = 32
UNROLL_LIMIT = 64


def repeat(count, body):
    if count <= UNROLL_LIMIT:
        for step in range(count):
            body(step)
    else:

        def rolled(step, carry):
            body(step)
            return carry

        lax.fori_loop(0, count, rolled, 0)


def kernel(
    seq_size,
    rep_size,
    q_hbm,
    k_hbm,
    v_hbm,
    sk_hbm,
    sv_hbm,
    owner_hbm,
    super_hbm,
    fine_hbm,
    out_ref,
    q_own,
    k_ref,
    v_ref,
    sk_ref,
    sv_ref,
    owner_ref,
    super_ref,
    fine_ref,
    q_all,
    parts,
    landed,
    in_sems,
    kv_sems,
    q_send,
    q_recv,
    p_send,
    p_recv,
):
    my_seq = lax.axis_index("seq")
    my_rep = lax.axis_index("rep")
    devices = seq_size * rep_size
    me = my_seq * rep_size + my_rep
    own_rows, heads, head_dim = q_own.shape
    groups, tokens = k_ref.shape[:2]
    per_group = heads // groups
    slot_count = owner_ref.shape[0]
    requests = parts.shape[0]
    out_rows = out_ref.shape[0]
    blocks = tokens // BLK

    small = [
        pltpu.make_async_copy(src, dst, in_sems.at[i])
        for i, (src, dst) in enumerate(
            (
                (q_hbm, q_own),
                (owner_hbm, owner_ref),
                (super_hbm, super_ref),
                (fine_hbm, fine_ref),
                (sk_hbm, sk_ref),
                (sv_hbm, sv_ref),
            )
        )
    ]
    for copy in small:
        copy.start()
    big = []
    for g in range(groups):
        big.append(
            (
                pltpu.make_async_copy(k_hbm.at[g], k_ref.at[g], kv_sems.at[0, g]),
                pltpu.make_async_copy(v_hbm.at[g], v_ref.at[g], kv_sems.at[1, g]),
            )
        )
    for pair in big:
        for copy in pair:
            copy.start()

    barrier = pltpu.get_barrier_semaphore()

    def greet(step):
        other = lax.rem(me + step + 1, devices)
        pl.semaphore_signal(
            barrier,
            inc=1,
            device_id=(lax.div(other, rep_size), lax.rem(other, rep_size)),
            device_id_type=pl.DeviceIdType.MESH,
        )

    repeat(devices - 1, greet)

    for copy in small:
        copy.wait()
    upper = lax.broadcasted_iota(jnp.int32, (heads, head_dim), 0) < per_group
    first, second = [], []
    for r in range(0, own_rows, 2):
        even = q_own[r].astype(jnp.float32)
        odd = q_own[r + 1].astype(jnp.float32)
        first.append(jnp.where(upper, even, pltpu.roll(odd, per_group, 0)))
        second.append(jnp.where(upper, pltpu.roll(even, per_group, 0), odd))
    q_all[my_seq, 0] = jnp.concatenate(first, axis=0).astype(jnp.bfloat16)
    q_all[my_seq, 1] = jnp.concatenate(second, axis=0).astype(jnp.bfloat16)

    pl.semaphore_wait(barrier, devices - 1)

    def send_queries(step):
        other = lax.rem(my_seq + step + 1, seq_size)
        pltpu.make_async_remote_copy(
            src_ref=q_all.at[my_seq],
            dst_ref=q_all.at[my_seq],
            send_sem=q_send,
            recv_sem=q_recv,
            device_id=(other, my_rep),
            device_id_type=pl.DeviceIdType.MESH,
        ).start()

    repeat(seq_size - 1, send_queries)

    if slot_count <= UNROLL_LIMIT:
        here = jnp.int32(0)
        for j in range(slot_count):
            here = here + jnp.where(owner_ref[j] == my_seq, j, 0)
    else:
        here = lax.fori_loop(
            0, slot_count, lambda j, total: total + jnp.where(owner_ref[j] == my_seq, j, 0), jnp.int32(0)
        )
    here = here.astype(jnp.float32)

    rows = CHUNK * per_group
    row_of = lax.broadcasted_iota(jnp.int32, (rows, CHUNK), 0)
    low = lax.broadcasted_iota(jnp.int32, (rows, CHUNK), 1) * per_group
    expand = jnp.where((row_of >= low) & (row_of < low + per_group), 1.0, 0.0).astype(jnp.bfloat16)
    scaling = head_dim ** (-0.5) * LOG2E

    def selection(chunk, g):
        picked = pl.ds(chunk * CHUNK, CHUNK)
        fine = fine_ref[picked, g, :].astype(jnp.float32).astype(jnp.bfloat16)
        supers = super_ref[picked, g, :].astype(jnp.float32).astype(jnp.bfloat16)
        fine = jnp.dot(expand, fine, preferred_element_type=jnp.float32)
        supers = jnp.dot(expand, supers, preferred_element_type=jnp.float32)
        place = lax.broadcasted_iota(jnp.int32, supers.shape, 1).astype(jnp.float32) + 1.0
        place = jnp.sum(jnp.where(supers == here, place, 0.0), axis=1, keepdims=True)
        at = (fine - SUPER * (place - 1.0)).astype(jnp.int32)
        valid = (at >= 0) & (at < SUPER) & (place > 0.0)
        bit = jnp.left_shift(1, jnp.clip(at, 0, SUPER - 1)).astype(jnp.float32)
        bits = jnp.sum(jnp.where(valid, bit, 0.0), axis=1, keepdims=True).astype(jnp.int32)
        return place, bits

    def attend(chunk, g, place, bits):
        sources = CHUNK // own_rows
        query = q_all[pl.ds(chunk * sources, sources), g].reshape(rows, head_dim)
        bits = jnp.broadcast_to(bits, (rows, BLK))
        scores = lax.dot_general(
            query, k_ref[g], (((1,), (1,)), ((), ())), preferred_element_type=jnp.float32
        )
        masked = []
        for b in range(blocks):
            one = scores[:, b * BLK : (b + 1) * BLK]
            masked.append(jnp.where((bits & (1 << b)) != 0, one, NEGATIVE))
        peak = functools.reduce(jnp.maximum, masked)
        peak = jnp.max(peak, axis=1, keepdims=True)
        weights = [jnp.exp2((one - peak) * scaling) for one in masked]
        total = jnp.sum(functools.reduce(jnp.add, weights), axis=1, keepdims=True)
        packed = jnp.concatenate([one.astype(jnp.bfloat16) for one in weights], axis=1)
        summed = jnp.dot(packed, v_ref[g], preferred_element_type=jnp.float32)
        coarse = jnp.sum(
            query.astype(jnp.float32) * sk_ref[g].astype(jnp.float32), axis=1, keepdims=True
        )
        coarse = coarse * scaling + math.log2(SUPER)
        stat = jnp.where(place > 0.0, peak * scaling + jnp.log2(total), coarse)
        value = jnp.where(place > 0.0, summed / total, sv_ref[g].astype(jnp.float32))
        return value, jnp.broadcast_to(stat, (rows, head_dim))

    def regroup(both):
        a, b = both
        pairs = rows // heads
        a = a.reshape(pairs, heads, head_dim)
        b = b.reshape(pairs, heads, head_dim)
        top = lax.broadcasted_iota(jnp.int32, a.shape, 1) < per_group
        even = jnp.where(top, a, pltpu.roll(b, per_group, 1))
        odd = jnp.where(top, pltpu.roll(a, per_group, 1), b)
        return even, odd

    def owner_chunk(chunk, chosen=None):
        if chosen is None:
            chosen = [selection(chunk, g) for g in range(groups)]
        results = [attend(chunk, g, *chosen[g]) for g in range(groups)]
        values = regroup([value for value, _ in results])
        stats = regroup([stat for _, stat in results])
        lane = lax.broadcasted_iota(jnp.int32, values[0].shape, 2)
        for which in range(2):
            stat = stats[which]
            high = stat.astype(jnp.bfloat16).astype(jnp.float32)
            rest = stat - high
            middle = rest.astype(jnp.bfloat16).astype(jnp.float32)
            last = rest - middle
            split = jnp.where(lane == 0, high, jnp.where(lane == 1, middle, jnp.where(lane == 2, last, 0.0)))
            message = jnp.concatenate([values[which], split], axis=1).astype(jnp.bfloat16)
            for pair in range(rows // heads):
                parts[chunk * CHUNK + 2 * pair + which] = message[pair]

    def wait_queries():
        got = q_all.at[pl.ds(0, seq_size - 1)]
        pltpu.make_async_copy(got, got, q_recv).wait()

    if requests == CHUNK:
        chosen = [selection(0, g) for g in range(groups)]
        for pair in big:
            for copy in pair:
                copy.wait()
        wait_queries()
        owner_chunk(0, chosen)
    else:
        for pair in big:
            for copy in pair:
                copy.wait()
        wait_queries()

        def chunk_step(chunk, carry):
            owner_chunk(chunk)
            return carry

        lax.fori_loop(0, requests // CHUNK, chunk_step, 0)

    def send_part(step):
        other = lax.rem(me + step + 1, devices)
        pltpu.make_async_remote_copy(
            src_ref=parts.at[pl.ds(other * out_rows, out_rows)],
            dst_ref=landed.at[me],
            send_sem=p_send,
            recv_sem=p_recv,
            device_id=(lax.div(other, rep_size), lax.rem(other, rep_size)),
            device_id_type=pl.DeviceIdType.MESH,
        ).start()

    repeat(devices - 1, send_part)
    landed[me] = parts[pl.ds(me * out_rows, out_rows)]
    got = landed.at[pl.ds(0, devices - 1)]
    pltpu.make_async_copy(got, got, p_recv).wait()

    for i in range(out_rows):
        for p in range(rep_size):
            stats, values = [], []
            for s in range(seq_size):
                message = landed[s * rep_size + p, i].astype(jnp.float32)
                values.append(message[:heads])
                stats.append(jnp.sum(message[heads:], axis=1, keepdims=True))
            peak = functools.reduce(jnp.maximum, stats)
            factors = [jnp.exp2(stat - peak) for stat in stats]
            total = functools.reduce(jnp.add, factors)
            summed = functools.reduce(jnp.add, [f * v for f, v in zip(factors, values)])
            out_ref[i, p * heads : (p + 1) * heads] = (summed / total).astype(out_ref.dtype)

    sent = q_all.at[pl.ds(0, seq_size - 1)]
    pltpu.make_async_copy(sent, sent, q_send).wait()
    sent = landed.at[pl.ds(0, devices - 1)]
    pltpu.make_async_copy(sent, sent, p_send).wait()


def solution(mesh):
    seq_size = mesh.shape["seq"]
    rep_size = mesh.shape["rep"]

    def shards(queries, key_cache, value_cache, summary_keys, summary_values, owner_map, super_ids, fine_ids):
        own_rows, heads, head_dim = queries.shape
        groups, tokens = key_cache.shape[:2]
        requests = super_ids.shape[0]
        devices = seq_size * rep_size
        out_rows = own_rows // rep_size
        assert summary_keys.shape[1] == 1 and tokens == SUPER * BLK
        assert groups == 2 and heads == 8 and own_rows % rep_size == 0 and own_rows % 2 == 0
        assert requests % CHUNK == 0 and CHUNK % own_rows == 0
        per_source = own_rows * heads // groups
        hbm = pl.BlockSpec(memory_space=pltpu.HBM)
        return pl.pallas_call(
            functools.partial(kernel, seq_size, rep_size),
            out_shape=jax.ShapeDtypeStruct((out_rows, rep_size * heads, head_dim), jnp.bfloat16),
            in_specs=[hbm] * 8,
            out_specs=pl.BlockSpec(memory_space=pltpu.VMEM),
            scratch_shapes=[
                pltpu.VMEM(queries.shape, queries.dtype),
                pltpu.VMEM(key_cache.shape, key_cache.dtype),
                pltpu.VMEM(value_cache.shape, value_cache.dtype),
                pltpu.VMEM(summary_keys.shape, summary_keys.dtype),
                pltpu.VMEM(summary_values.shape, summary_values.dtype),
                pltpu.SMEM(owner_map.shape, owner_map.dtype),
                pltpu.VMEM(super_ids.shape, super_ids.dtype),
                pltpu.VMEM(fine_ids.shape, fine_ids.dtype),
                pltpu.VMEM((seq_size, groups, per_source, head_dim), jnp.bfloat16),
                pltpu.VMEM((requests, 2 * heads, head_dim), jnp.bfloat16),
                pltpu.VMEM((devices, out_rows, 2 * heads, head_dim), jnp.bfloat16),
                pltpu.SemaphoreType.DMA((6,)),
                pltpu.SemaphoreType.DMA((2, groups)),
                pltpu.SemaphoreType.DMA,
                pltpu.SemaphoreType.DMA,
                pltpu.SemaphoreType.DMA,
                pltpu.SemaphoreType.DMA,
            ],
            compiler_params=pltpu.CompilerParams(collective_id=0, has_side_effects=True),
        )(queries, key_cache, value_cache, summary_keys, summary_values, owner_map, super_ids, fine_ids)

    in_specs = (
        P("seq", "rep", None),
        P("rep", "seq", None),
        P("rep", "seq", None),
        P("rep", "seq", None),
        P("rep", "seq", None),
        P(),
        P(None, "rep", None),
        P(None, "rep", None),
    )
    out_specs = P(("seq", "rep"), None, None)
    return jax.shard_map(shards, mesh=mesh, in_specs=in_specs, out_specs=out_specs, check_vma=False)
```

time: 79.1 us -> 23.1 us (0.29)
  blocking collectives: 38.9 us -> 0 us
  Pallas kernels: 0 us -> 17.6 us
  waiting for transfers between devices: 16.9 us -> 0 us
  starting transfers between devices: 12.2 us -> 0 us
  other arithmetic: 3.39 us -> 0 us
  matrix products: 3.23 us -> 0 us
  local copies, waits for them, and re-layouts: 3.75 us -> 5.19 us
    all_gather x1 -> x0, blocking collectives: 32.6 us -> none  [shards(): everyone = lax.all_gather(queries, 'seq', axis=0, tiled=True)]
    pallas_call x0 -> x1, Pallas kernels: none -> 17.6 us  [shards(): pl.pallas_call(functools.partial(kernel, seq_size, rep_size), out_shape=j...]
    all_to_all x3 -> x0, waiting for transfers between devices: 16.9 us -> none  [the longest x1 6.62 us: shards(): lax.all_to_all(weighted, 'seq', split_axis=0, concat_axis=0, tiled=True)]
    all_to_all x3 -> x0, starting transfers between devices: 12.2 us -> none  [the longest x1 5.49 us: shards(): lax.all_to_all(highest, 'seq', split_axis=0, concat_axis=0, tiled=True)]
    all_to_all x1 -> x0, blocking collectives: 6.37 us -> none  [shards(): lax.all_to_all(result, 'rep', split_axis=0, concat_axis=1, tiled=True)]
    unnamed x6 -> x9, local copies, waits for them, and re-layouts: 0.71 us -> 5.19 us
    dot_general x3 -> x0, matrix products: 3.23 us -> none  [the longest x1 1.83 us: fine_terms(): jnp.einsum('bgqt,gtd->bgqd', weights.reshape(row_count, groups, per_group...]
    reduce_sum x5 -> x0, other arithmetic: 1.64 us -> none  [the longest x1 0.88 us: shards(): slots = jnp.sum(jnp.where(is_super, owner_map, 0), axis=3)]
  transfers between devices with their start and end apart: 3 -> 0, of which waited for: 3 -> 0; matrix products, arithmetic and copies ran while one was open for 5% -> 0% of each run, Pallas kernels for 0% -> 0%
where the time goes in v1:
time: 23.1 us; the launch traced here: 22.8 us
  Pallas kernels  17.6 us (76%)
  local copies, waits for them, and re-layouts  5.19 us (22%)
    pallas_call x1, Pallas kernels, shards(): pl.pallas_call(functools.partial(kernel, seq_size, rep_size), out_shape=j...  17.6 us
    unnamed x9, local copies, waits for them, and re-layouts  5.19 us

profile of v1, /device:TPU:0, one launch (start us, length us, event | category | flops | bytes accessed | tf_op | source)
XLA Modules:
  0.0 22.8 jit_solution(14790948267327240715)
XLA Ops:
  0.0 0.0 copy-start.1
  0.0 1.2 %copy.9.sk_hbm = bf16[2,1,128]{2,1,0:T(2,128)(2,1)} copy(bf16[2,1,128]{2,0,1:T(2,128)(2,1)} %param.11) | data formatting | bytes 1024 | tf_op args[3]
  1.2 0.0 copy-done.1
  1.2 0.6 %copy.10.sv_hbm = bf16[2,1,128]{2,1,0:T(2,128)(2,1)} copy(bf16[2,1,128]{2,0,1:T(2,128)(2,1)S(1)} %copy-done.1) | data formatting | bytes 1024 | tf_op args[4]
  1.8 0.0 copy-start
  1.8 1.4 %copy.11.super_hbm = s32[32,2,4]{2,1,0:T(2,128)} copy(s32[32,2,4]{0,2,1:T(4,128)} %param.14) | data formatting | bytes 2048 | tf_op args[6]
  3.2 0.0 copy-done
  3.2 0.7 %copy.12.fine_hbm = s32[32,2,16]{2,1,0:T(2,128)} copy(s32[32,2,16]{0,2,1:T(8,128)S(1)} %copy-done) | data formatting | bytes 8192 | tf_op args[7]
  3.9 17.6 %shard_map.82 = bf16[1,32,128]{2,1,0:T(8,128)(2,1)} custom-call(bf16[4,8,128]{2,1,0:T(8,128)(2,1)} %q_hbm.1, bf16[2,2048,128]{2,1,0:T(8,128)(2,1)} %k_hbm.1, bf16[2,2048,128]{2,1,0:T(8,128)(2,1)} %v_hbm.1, bf16[2,1,128]{2,1,0:T(2,128)(2,1)} %copy.9.sk_hbm, bf16[2,1,128]{2,1,0:T(2,128)(2,1)} %copy.10.sv_hbm, s32[8]{0:T(128)} %owner_hbm.1, ...), custom_call_target="tpu_custom_call" | custom-call | tf_op jit(solution)/shard_map/pallas_call | solution.py:297
  21.5 1.3 %copy.14 = bf16[1,32,128]{2,1,0:T(8,128)(2,1)} copy(bf16[1,32,128]{2,1,0:T(8,128)(2,1)} %shard_map.82) | data formatting | bytes 16384
Async XLA Ops:
  0.0 1.2 %copy-start.1 = (bf16[2,1,128]{2,0,1:T(2,128)(2,1)S(1)}, bf16[2,1,128]{2,0,1:T(2,128)(2,1)}, u32[]{:S(2)}) copy-start(bf16[2,1,128]{2,0,1:T(2,128)(2,1)} %param.12) | copy-start | bytes 1540
  1.8 1.4 %copy-start = (s32[32,2,16]{0,2,1:T(8,128)S(1)}, s32[32,2,16]{0,2,1:T(8,128)}, u32[]{:S(2)}) copy-start(s32[32,2,16]{0,2,1:T(8,128)} %param.15) | copy-start | bytes 12292

commit v2 on v1

v2 whole, which is shorter than its diff:
```python
import functools
import math

import jax
import jax.numpy as jnp
from jax import lax
from jax.experimental import pallas as pl
from jax.experimental.pallas import tpu as pltpu
from jax.sharding import PartitionSpec as P

BLK = 128
SUPER = 16
NEGATIVE = -1e30
LOG2E = math.log2(math.e)
CHUNK = 32
WIDTH = 16
UNROLL_LIMIT = 64


def repeat(count, body):
    if count <= UNROLL_LIMIT:
        for step in range(count):
            body(step)
    else:

        def rolled(step, carry):
            body(step)
            return carry

        lax.fori_loop(0, count, rolled, 0)


def kernel(
    seq_size,
    rep_size,
    q_hbm,
    k_hbm,
    v_hbm,
    sk_hbm,
    sv_hbm,
    owner_hbm,
    super_hbm,
    fine_hbm,
    out_ref,
    k_ref,
    v_ref,
    sk_ref,
    sv_ref,
    owner_ref,
    super_ref,
    fine_ref,
    q_all,
    part_values,
    part_stats,
    landed_values,
    landed_stats,
    in_sems,
    kv_sems,
    q_send,
    q_recv,
    p_send,
    p_recv,
):
    my_seq = lax.axis_index("seq")
    my_rep = lax.axis_index("rep")
    devices = seq_size * rep_size
    own_rows, heads, head_dim = q_hbm.shape
    groups, tokens = k_ref.shape[:2]
    per_group = heads // groups
    slot_count = owner_ref.shape[0]
    out_rows = out_ref.shape[0]
    blocks = tokens // BLK
    near = q_recv.shape[0]
    sources = seq_size // near
    width = sources * own_rows
    my_block = lax.div(my_seq, sources)
    my_place = lax.rem(my_seq, sources)

    barrier = pltpu.get_barrier_semaphore()

    def reach(seq, rep):
        return dict(device_id=(seq, rep), device_id_type=pl.DeviceIdType.MESH)

    def greet_seq(step):
        pl.semaphore_signal(barrier, inc=1, **reach(lax.rem(my_seq + step + 1, seq_size), my_rep))

    def greet_rep(step):
        pl.semaphore_signal(barrier, inc=1, **reach(my_seq, lax.rem(my_rep + step + 1, rep_size)))

    repeat(seq_size - 1, greet_seq)
    repeat(rep_size - 1, greet_rep)

    mine = q_all.at[pl.ds(my_seq * own_rows, own_rows)]
    small = [
        pltpu.make_async_copy(src, dst, in_sems.at[i])
        for i, (src, dst) in enumerate(
            (
                (q_hbm, mine),
                (owner_hbm, owner_ref),
                (super_hbm, super_ref),
                (fine_hbm, fine_ref),
                (sk_hbm, sk_ref),
                (sv_hbm, sv_ref),
            )
        )
    ]
    for copy in small:
        copy.start()
    big = []
    for g in range(groups):
        big.append(pltpu.make_async_copy(k_hbm.at[g], k_ref.at[g], kv_sems.at[0, g]))
        big.append(pltpu.make_async_copy(v_hbm.at[g], v_ref.at[g], kv_sems.at[1, g]))
    for copy in big:
        copy.start()

    pl.semaphore_wait(barrier, seq_size - 1 + rep_size - 1)

    def send_query(away, place):
        block = lax.rem(my_block + away, near)
        pltpu.make_async_remote_copy(
            src_ref=q_hbm,
            dst_ref=mine,
            send_sem=q_send,
            recv_sem=q_recv.at[(near - away) % near],
            **reach(block * sources + place, my_rep),
        ).start()

    def send_block(step):
        away = near - 1 - step
        for place in range(sources):
            send_query(away, lax.rem(my_place + place, sources))

    repeat(near - 1, send_block)
    for place in range(1, sources):
        send_query(0, lax.rem(my_place + place, sources))

    for copy in small:
        copy.wait()

    if slot_count <= UNROLL_LIMIT:
        here = jnp.int32(0)
        for j in range(slot_count):
            here = here + jnp.where(owner_ref[j] == my_seq, j, 0)
    else:
        here = lax.fori_loop(
            0, slot_count, lambda j, total: total + jnp.where(owner_ref[j] == my_seq, j, 0), jnp.int32(0)
        )
    here = here.astype(jnp.float32)

    rows = width * per_group
    pairs = width // 2
    row_of = lax.broadcasted_iota(jnp.int32, (rows, CHUNK), 0)
    lane_of = lax.broadcasted_iota(jnp.int32, (rows, CHUNK), 1)
    scaling = head_dim ** (-0.5) * LOG2E
    sub = lax.broadcasted_iota(jnp.int32, (pairs, heads, head_dim), 1)
    lane = lax.broadcasted_iota(jnp.int32, (pairs, heads, head_dim), 2)
    top = sub < per_group
    diagonal = sub == lane

    def selection(first, g):
        chunk = lax.div(first, CHUNK)
        low = (lane_of - lax.rem(first, CHUNK)) * per_group
        expand = jnp.where((row_of >= low) & (row_of < low + per_group), 1.0, 0.0).astype(jnp.bfloat16)
        fine = fine_ref[chunk, g].astype(jnp.float32).astype(jnp.bfloat16)
        supers = super_ref[chunk, g].astype(jnp.float32).astype(jnp.bfloat16)
        contract = (((1,), (1,)), ((), ()))
        fine = lax.dot_general(expand, fine, contract, preferred_element_type=jnp.float32)
        supers = lax.dot_general(expand, supers, contract, preferred_element_type=jnp.float32)
        place = lax.broadcasted_iota(jnp.int32, supers.shape, 1).astype(jnp.float32) + 1.0
        place = jnp.sum(jnp.where(supers == here, place, 0.0), axis=1, keepdims=True)
        at = (fine - SUPER * (place - 1.0)).astype(jnp.int32)
        valid = (at >= 0) & (at < SUPER) & (place > 0.0)
        bit = jnp.left_shift(1, jnp.clip(at, 0, SUPER - 1)).astype(jnp.float32)
        bits = jnp.sum(jnp.where(valid, bit, 0.0), axis=1, keepdims=True).astype(jnp.int32)
        return place, bits

    def regroup(a, b):
        return jnp.where(top, a, pltpu.roll(b, per_group, 1)), jnp.where(top, pltpu.roll(a, per_group, 1), b)

    def attend(query, g, place, bits):
        bits = jnp.broadcast_to(bits, (rows, BLK))
        scores = lax.dot_general(
            query.astype(jnp.bfloat16), k_ref[g], (((1,), (1,)), ((), ())), preferred_element_type=jnp.float32
        )
        masked = []
        for b in range(blocks):
            one = scores[:, b * BLK : (b + 1) * BLK]
            masked.append(jnp.where((bits & (1 << b)) != 0, one, NEGATIVE))
        peak = functools.reduce(jnp.maximum, masked)
        peak = jnp.max(peak, axis=1, keepdims=True)
        weights = [jnp.exp2((one - peak) * scaling) for one in masked]
        total = jnp.sum(functools.reduce(jnp.add, weights), axis=1, keepdims=True)
        packed = jnp.concatenate([one.astype(jnp.bfloat16) for one in weights], axis=1)
        summed = jnp.dot(packed, v_ref[g], preferred_element_type=jnp.float32)
        coarse = jnp.sum(query * sk_ref[:, g].astype(jnp.float32), axis=1, keepdims=True)
        coarse = coarse * scaling + math.log2(SUPER)
        stat = jnp.where(place > 0.0, peak * scaling + jnp.log2(total), coarse)
        value = jnp.where(place > 0.0, summed / total, sv_ref[:, g].astype(jnp.float32))
        stat = jnp.broadcast_to(stat, (rows, head_dim))
        return value.reshape(pairs, heads, head_dim), stat.reshape(pairs, heads, head_dim)

    def block_parts(first, chosen):
        raw = q_all[pl.ds(first, width)].astype(jnp.float32).reshape(pairs, 2, heads, head_dim)
        queries = [one.reshape(rows, head_dim) for one in regroup(raw[:, 0], raw[:, 1])]
        (value_a, stat_a), (value_b, stat_b) = [attend(queries[g], g, *chosen[g]) for g in range(groups)]
        values = [one.astype(jnp.bfloat16) for one in regroup(value_a, value_b)]
        stats = [
            jnp.sum(jnp.where(diagonal, one, 0.0), axis=1, keepdims=True) for one in regroup(stat_a, stat_b)
        ]
        for which in range(2):
            for pair in range(pairs):
                part_values[first + 2 * pair + which] = values[which][pair]
                part_stats[first + 2 * pair + which] = stats[which][pair]

    slot = pl.ds(my_rep * seq_size + my_seq, 1)
    messages = ((part_values, landed_values), (part_stats, landed_stats))

    def send_parts(first, start, skip):
        targets = width // out_rows
        for step in range(skip, targets):
            target = lax.rem(start + step, targets)
            there = lax.div(first, out_rows) + target
            for kind, (source, landed) in enumerate(messages):
                pltpu.make_async_remote_copy(
                    src_ref=source.at[pl.ds(first + target * out_rows, out_rows)],
                    dst_ref=landed.at[my_rep * seq_size + my_seq],
                    send_sem=p_send.at[kind],
                    recv_sem=p_recv.at[kind],
                    **reach(lax.div(there, rep_size), lax.rem(there, rep_size)),
                ).start()

    def wait_block(away, count):
        got = q_all.at[pl.ds(0, count * own_rows)]
        pltpu.make_async_copy(got, got, q_recv.at[away]).wait()

    def block_first(away):
        return lax.rem(my_block + away, near) * width

    mine_at = my_place * rep_size + my_rep

    def run_block(away, chosen):
        wait_block(away, sources)
        block_parts(block_first(away), chosen)
        send_parts(block_first(away), mine_at, 0)

    def choose(away):
        return [selection(block_first(away), g) for g in range(groups)]

    ahead = [choose(away) for away in range(near)] if near <= 2 else None
    for copy in big:
        copy.wait()
    if sources > 1:
        wait_block(0, sources - 1)
    block_parts(block_first(0), ahead[0] if ahead else choose(0))
    send_parts(block_first(0), mine_at, 1)
    own = block_first(0) + mine_at * out_rows
    landed_values[slot] = part_values[pl.ds(own, out_rows)][None]
    landed_stats[slot] = part_stats[pl.ds(own, out_rows)][None]

    if ahead:
        for away in range(1, near):
            run_block(away, ahead[away])
    else:

        def block_step(away, carry):
            run_block(away, choose(away))
            return carry

        lax.fori_loop(1, near, block_step, 0)

    for kind, (_, landed) in enumerate(messages):
        got = landed.at[pl.ds(0, devices - 1)]
        pltpu.make_async_copy(got, got, p_recv.at[kind]).wait()

    same = lax.broadcasted_iota(jnp.int32, (heads, head_dim), 0) == lax.broadcasted_iota(
        jnp.int32, (heads, head_dim), 1
    )
    for i in range(out_rows):
        for p in range(rep_size):
            stats = [landed_stats[p * seq_size + s, i] for s in range(seq_size)]
            peak = functools.reduce(jnp.maximum, stats)
            factors = [jnp.exp2(stat - peak) for stat in stats]
            total = functools.reduce(jnp.add, factors)
            summed = jnp.zeros((heads, head_dim), jnp.float32)
            for s in range(seq_size):
                share = jnp.where(same, factors[s] / total, 0.0)
                share = jnp.sum(share, axis=1, keepdims=True)
                summed = summed + share * landed_values[p * seq_size + s, i].astype(jnp.float32)
            out_ref[i, p * heads : (p + 1) * heads] = summed.astype(out_ref.dtype)

    sent = q_all.at[pl.ds(0, (seq_size - 1) * own_rows)]
    pltpu.make_async_copy(sent, sent, q_send).wait()
    for kind, (_, landed) in enumerate(messages):
        sent = landed.at[pl.ds(0, devices - 1)]
        pltpu.make_async_copy(sent, sent, p_send.at[kind]).wait()


def solution(mesh):
    seq_size = mesh.shape["seq"]
    rep_size = mesh.shape["rep"]

    def shards(queries, key_cache, value_cache, summary_keys, summary_values, owner_map, super_ids, fine_ids):
        own_rows, heads, head_dim = queries.shape
        groups, tokens = key_cache.shape[:2]
        requests = super_ids.shape[0]
        devices = seq_size * rep_size
        out_rows = own_rows // rep_size
        sources = math.gcd(seq_size, max(WIDTH // own_rows, 1))
        assert summary_keys.shape[1] == 1 and tokens == SUPER * BLK
        assert groups == 2 and heads == 8 and own_rows % rep_size == 0 and own_rows % 2 == 0
        assert requests % CHUNK == 0 and CHUNK % (sources * own_rows) == 0
        hbm = pl.BlockSpec(memory_space=pltpu.HBM)
        summary_keys = jnp.transpose(summary_keys, (1, 0, 2))
        summary_values = jnp.transpose(summary_values, (1, 0, 2))
        chunked = (requests // CHUNK, CHUNK, groups, -1)
        super_ids = jnp.transpose(super_ids.reshape(chunked), (0, 2, 3, 1))
        fine_ids = jnp.transpose(fine_ids.reshape(chunked), (0, 2, 3, 1))
        return pl.pallas_call(
            functools.partial(kernel, seq_size, rep_size),
            out_shape=pltpu.VMEM((out_rows, rep_size * heads, head_dim), jnp.bfloat16),
            in_specs=[hbm] * 8,
            out_specs=pl.BlockSpec(memory_space=pltpu.VMEM),
            scratch_shapes=[
                pltpu.VMEM(key_cache.shape, key_cache.dtype),
                pltpu.VMEM(value_cache.shape, value_cache.dtype),
                pltpu.VMEM(summary_keys.shape, summary_keys.dtype),
                pltpu.VMEM(summary_values.shape, summary_values.dtype),
                pltpu.SMEM(owner_map.shape, owner_map.dtype),
                pltpu.VMEM(super_ids.shape, super_ids.dtype),
                pltpu.VMEM(fine_ids.shape, fine_ids.dtype),
                pltpu.VMEM((seq_size * own_rows, heads, head_dim), jnp.bfloat16),
                pltpu.VMEM((requests, heads, head_dim), jnp.bfloat16),
                pltpu.VMEM((requests, 1, head_dim), jnp.float32),
                pltpu.VMEM((devices, out_rows, heads, head_dim), jnp.bfloat16),
                pltpu.VMEM((devices, out_rows, 1, head_dim), jnp.float32),
                pltpu.SemaphoreType.DMA((6,)),
                pltpu.SemaphoreType.DMA((2, groups)),
                pltpu.SemaphoreType.DMA,
                pltpu.SemaphoreType.DMA((seq_size // sources,)),
                pltpu.SemaphoreType.DMA((2,)),
                pltpu.SemaphoreType.DMA((2,)),
            ],
            compiler_params=pltpu.CompilerParams(collective_id=0, has_side_effects=True),
        )(queries, key_cache, value_cache, summary_keys, summary_values, owner_map, super_ids, fine_ids)

    in_specs = (
        P("seq", "rep", None),
        P("rep", "seq", None),
        P("rep", "seq", None),
        P("rep", "seq", None),
        P("rep", "seq", None),
        P(),
        P(None, "rep", None),
        P(None, "rep", None),
    )
    out_specs = P(("seq", "rep"), None, None)
    return jax.shard_map(shards, mesh=mesh, in_specs=in_specs, out_specs=out_specs, check_vma=False)
```

time: 23.1 us -> 17.7 us (0.77)
  local copies, waits for them, and re-layouts: 5.19 us -> 0.6 us
  Pallas kernels: 17.6 us -> 16.9 us
    unnamed x9 -> x1, local copies, waits for them, and re-layouts: 5.19 us -> 0.6 us
    pallas_call x1, Pallas kernels: 17.6 us -> 16.9 us  [shards(): pl.pallas_call(functools.partial(kernel, seq_size, rep_size), out_shape=p...]
where the time goes in v2:
time: 17.7 us; the launch traced here: 17.5 us
  Pallas kernels  16.9 us (95%)
  local copies, waits for them, and re-layouts  0.6 us (3%)
    pallas_call x1, Pallas kernels, shards(): pl.pallas_call(functools.partial(kernel, seq_size, rep_size), out_shape=p...  16.9 us
    unnamed x1, local copies, waits for them, and re-layouts  0.6 us

profile of v2, /device:TPU:0, one launch (start us, length us, event | category | flops | bytes accessed | tf_op | source)
XLA Modules:
  0.0 17.5 jit_solution(13452451934944215894)
XLA Ops:
  0.0 16.9 %shard_map.82 = bf16[1,32,128]{2,1,0:T(8,128)(2,1)S(1)} custom-call(bf16[4,8,128]{2,1,0:T(8,128)(2,1)} %q_hbm.1, bf16[2,2048,128]{2,1,0:T(8,128)(2,1)} %k_hbm.1, bf16[2,2048,128]{2,1,0:T(8,128)(2,1)} %v_hbm.1, bf16[1,2,128]{2,1,0:T(2,128)(2,1)} %bitcast.10, bf16[1,2,128]{2,1,0:T(2,128)(2,1)} %bitcast.11, s32[8]{0:T(128)} %owner_hbm.1, ...), custom_call_target="tpu_custom_call" | custom-call | tf_op jit(solution)/shard_map/pallas_call | solution.py:318
  16.9 0.6 %copy.10 = bf16[1,32,128]{2,1,0:T(8,128)(2,1)} copy(bf16[1,32,128]{2,1,0:T(8,128)(2,1)S(1)} %shard_map.82) | data formatting | bytes 16384

commit v3 on v2

--- a/solution.py
+++ b/solution.py
@@ -13,7 +13,7 @@
 NEGATIVE = -1e30
 LOG2E = math.log2(math.e)
 CHUNK = 32
-WIDTH = 16
+NEAR = 4
 UNROLL_LIMIT = 64
 
 
@@ -57,7 +57,8 @@
     in_sems,
     kv_sems,
     q_send,
-    q_recv,
+    q_far,
+    q_near,
     p_send,
     p_recv,
 ):
@@ -70,9 +71,10 @@
     slot_count = owner_ref.shape[0]
     out_rows = out_ref.shape[0]
     blocks = tokens // BLK
-    near = q_recv.shape[0]
+    near = q_far.shape[0]
     sources = seq_size // near
-    width = sources * own_rows
+    width = CHUNK
+    chunks = q_all.shape[0] // CHUNK
     my_block = lax.div(my_seq, sources)
     my_place = lax.rem(my_seq, sources)
 
@@ -81,13 +83,23 @@
     def reach(seq, rep):
         return dict(device_id=(seq, rep), device_id_type=pl.DeviceIdType.MESH)
 
-    def greet_seq(step):
-        pl.semaphore_signal(barrier, inc=1, **reach(lax.rem(my_seq + step + 1, seq_size), my_rep))
+    def same_block(step):
+        return my_block * sources + lax.rem(my_place + step, sources)
+
+    def same_place(step):
+        return lax.rem(my_block + step, near) * sources + my_place
+
+    def greet_near(step):
+        pl.semaphore_signal(barrier, inc=1, **reach(same_block(step + 1), my_rep))
+
+    def greet_far(step):
+        pl.semaphore_signal(barrier, inc=1, **reach(same_place(step + 1), my_rep))
 
     def greet_rep(step):
         pl.semaphore_signal(barrier, inc=1, **reach(my_seq, lax.rem(my_rep + step + 1, rep_size)))
 
-    repeat(seq_size - 1, greet_seq)
+    repeat(near - 1, greet_far)
+    repeat(sources - 1, greet_near)
     repeat(rep_size - 1, greet_rep)
 
     mine = q_all.at[pl.ds(my_seq * own_rows, own_rows)]
@@ -113,28 +125,28 @@
     for copy in big:
         copy.start()
 
-    pl.semaphore_wait(barrier, seq_size - 1 + rep_size - 1)
-
-    def send_query(away, place):
-        block = lax.rem(my_block + away, near)
+    pl.semaphore_wait(barrier, near - 1 + sources - 1 + rep_size - 1)
+
+    def send_far(step):
         pltpu.make_async_remote_copy(
             src_ref=q_hbm,
             dst_ref=mine,
-            send_sem=q_send,
-            recv_sem=q_recv.at[(near - away) % near],
-            **reach(block * sources + place, my_rep),
+            send_sem=q_send.at[0],
+            recv_sem=q_far.at[(near - 1 - step) % near],
+            **reach(same_place(step + 1), my_rep),
         ).start()
 
-    def send_block(step):
-        away = near - 1 - step
-        for place in range(sources):
-            send_query(away, lax.rem(my_place + place, sources))
-
-    repeat(near - 1, send_block)
-    for place in range(1, sources):
-        send_query(0, lax.rem(my_place + place, sources))
-
-    for copy in small:
+    repeat(near - 1, send_far)
+    for step in range(1, sources):
+        pltpu.make_async_remote_copy(
+            src_ref=q_hbm,
+            dst_ref=mine,
+            send_sem=q_send.at[0],
+            recv_sem=q_near,
+            **reach(same_block(step), my_rep),
+        ).start()
+
+    for copy in small[1:]:
         copy.wait()
 
     if slot_count <= UNROLL_LIMIT:
@@ -229,44 +241,49 @@
                     **reach(lax.div(there, rep_size), lax.rem(there, rep_size)),
                 ).start()
 
-    def wait_block(away, count):
-        got = q_all.at[pl.ds(0, count * own_rows)]
-        pltpu.make_async_copy(got, got, q_recv.at[away]).wait()
-
-    def block_first(away):
-        return lax.rem(my_block + away, near) * width
-
-    mine_at = my_place * rep_size + my_rep
-
-    def run_block(away, chosen):
-        wait_block(away, sources)
-        block_parts(block_first(away), chosen)
-        send_parts(block_first(away), mine_at, 0)
-
-    def choose(away):
-        return [selection(block_first(away), g) for g in range(groups)]
-
-    ahead = [choose(away) for away in range(near)] if near <= 2 else None
+    def choose(first):
+        return [selection(first, g) for g in range(groups)]
+
+    my_chunk = lax.div(my_seq * own_rows, CHUNK)
+    ahead = choose(my_chunk * CHUNK)
+
+    def forward(step):
+        held = q_all.at[pl.ds(same_place(step + 1) * own_rows, own_rows)]
+        pltpu.make_async_copy(held, held, q_far.at[step + 1]).wait()
+        for place in range(1, sources):
+            pltpu.make_async_remote_copy(
+                src_ref=held,
+                dst_ref=held,
+                send_sem=q_send.at[1],
+                recv_sem=q_near,
+                **reach(same_block(place), my_rep),
+            ).start()
+
+    repeat(near - 1, forward)
+    small[0].wait()
     for copy in big:
         copy.wait()
+    passed = (sources - 1) * near * own_rows
     if sources > 1:
-        wait_block(0, sources - 1)
-    block_parts(block_first(0), ahead[0] if ahead else choose(0))
-    send_parts(block_first(0), mine_at, 1)
-    own = block_first(0) + mine_at * out_rows
+        got = q_all.at[pl.ds(0, passed)]
+        pltpu.make_async_copy(got, got, q_near).wait()
+
+    own = (my_seq * rep_size + my_rep) * out_rows
+    mine_at = lax.rem(my_seq * own_rows, CHUNK) // out_rows + my_rep
+    block_parts(my_chunk * CHUNK, ahead)
+    send_parts(my_chunk * CHUNK, mine_at, 1)
     landed_values[slot] = part_values[pl.ds(own, out_rows)][None]
     landed_stats[slot] = part_stats[pl.ds(own, out_rows)][None]
 
-    if ahead:
-        for away in range(1, near):
-            run_block(away, ahead[away])
-    else:
-
-        def block_step(away, carry):
-            run_block(away, choose(away))
+    if chunks > 1:
+
+        def chunk_step(step, carry):
+            first = lax.rem(my_chunk + step, chunks) * CHUNK
+            block_parts(first, choose(first))
+            send_parts(first, mine_at, 0)
             return carry
 
-        lax.fori_loop(1, near, block_step, 0)
+        lax.fori_loop(1, chunks, chunk_step, 0)
 
     for kind, (_, landed) in enumerate(messages):
         got = landed.at[pl.ds(0, devices - 1)]
@@ -288,8 +305,10 @@
                 summed = summed + share * landed_values[p * seq_size + s, i].astype(jnp.float32)
             out_ref[i, p * heads : (p + 1) * heads] = summed.astype(out_ref.dtype)
 
-    sent = q_all.at[pl.ds(0, (seq_size - 1) * own_rows)]
-    pltpu.make_async_copy(sent, sent, q_send).wait()
+    for i, count in enumerate((near - 1 + sources - 1, (near - 1) * (sources - 1))):
+        if count > 0:
+            sent = q_all.at[pl.ds(0, count * own_rows)]
+            pltpu.make_async_copy(sent, sent, q_send.at[i]).wait()
     for kind, (_, landed) in enumerate(messages):
         sent = landed.at[pl.ds(0, devices - 1)]
         pltpu.make_async_copy(sent, sent, p_send.at[kind]).wait()
@@ -305,10 +324,10 @@
         requests = super_ids.shape[0]
         devices = seq_size * rep_size
         out_rows = own_rows // rep_size
-        sources = math.gcd(seq_size, max(WIDTH // own_rows, 1))
+        sources = math.gcd(seq_size, NEAR)
         assert summary_keys.shape[1] == 1 and tokens == SUPER * BLK
         assert groups == 2 and heads == 8 and own_rows % rep_size == 0 and own_rows % 2 == 0
-        assert requests % CHUNK == 0 and CHUNK % (sources * own_rows) == 0
+        assert requests % CHUNK == 0 and CHUNK % own_rows == 0
         hbm = pl.BlockSpec(memory_space=pltpu.HBM)
         summary_keys = jnp.transpose(summary_keys, (1, 0, 2))
         summary_values = jnp.transpose(summary_values, (1, 0, 2))
@@ -335,8 +354,9 @@
                 pltpu.VMEM((devices, out_rows, 1, head_dim), jnp.float32),
                 pltpu.SemaphoreType.DMA((6,)),
                 pltpu.SemaphoreType.DMA((2, groups)),
+                pltpu.SemaphoreType.DMA((2,)),
+                pltpu.SemaphoreType.DMA((seq_size // sources,)),
                 pltpu.SemaphoreType.DMA,
-                pltpu.SemaphoreType.DMA((seq_size // sources,)),
                 pltpu.SemaphoreType.DMA((2,)),
                 pltpu.SemaphoreType.DMA((2,)),
             ],

time: 17.7 us -> 18.3 us (1.034)
  Pallas kernels: 16.9 us -> 17.6 us
    pallas_call x1, Pallas kernels: 16.9 us -> 17.6 us  [shards(): pl.pallas_call(functools.partial(kernel, seq_size, rep_size), out_shape=p...]
where the time goes in v3:
time: 18.3 us; the launch traced here: 18.2 us
  Pallas kernels  17.6 us (96%)
  local copies, waits for them, and re-layouts  0.6 us (3%)
    pallas_call x1, Pallas kernels, shards(): pl.pallas_call(functools.partial(kernel, seq_size, rep_size), out_shape=p...  17.6 us
    unnamed x1, local copies, waits for them, and re-layouts  0.6 us

profile of v3, /device:TPU:0, one launch (start us, length us, event | category | flops | bytes accessed | tf_op | source)
XLA Modules:
  0.0 18.2 jit_solution(12489303480888454061)
XLA Ops:
  0.0 17.6 %shard_map.82 = bf16[1,32,128]{2,1,0:T(8,128)(2,1)S(1)} custom-call(bf16[4,8,128]{2,1,0:T(8,128)(2,1)} %q_hbm.1, bf16[2,2048,128]{2,1,0:T(8,128)(2,1)} %k_hbm.1, bf16[2,2048,128]{2,1,0:T(8,128)(2,1)} %v_hbm.1, bf16[1,2,128]{2,1,0:T(2,128)(2,1)} %bitcast.10, bf16[1,2,128]{2,1,0:T(2,128)(2,1)} %bitcast.11, s32[8]{0:T(128)} %owner_hbm.1, ...), custom_call_target="tpu_custom_call" | custom-call | tf_op jit(solution)/shard_map/pallas_call | solution.py:337
  17.6 0.6 %copy.10 = bf16[1,32,128]{2,1,0:T(8,128)(2,1)} copy(bf16[1,32,128]{2,1,0:T(8,128)(2,1)S(1)} %shard_map.82) | data formatting | bytes 16384

commit v4 on v2

--- a/solution.py
+++ b/solution.py
@@ -13,7 +13,7 @@
 NEGATIVE = -1e30
 LOG2E = math.log2(math.e)
 CHUNK = 32
-WIDTH = 16
+WIDTH = 32
 UNROLL_LIMIT = 64
 
 

time: 17.7 us -> 18 us (1.017)
  Pallas kernels: 16.9 us -> 17.3 us
    pallas_call x1, Pallas kernels: 16.9 us -> 17.3 us  [shards(): pl.pallas_call(functools.partial(kernel, seq_size, rep_size), out_shape=p...]
where the time goes in v4:
time: 18 us; the launch traced here: 17.9 us
  Pallas kernels  17.3 us (96%)
  local copies, waits for them, and re-layouts  0.6 us (3%)
    pallas_call x1, Pallas kernels, shards(): pl.pallas_call(functools.partial(kernel, seq_size, rep_size), out_shape=p...  17.3 us
    unnamed x1, local copies, waits for them, and re-layouts  0.6 us

profile of v4, /device:TPU:0, one launch (start us, length us, event | category | flops | bytes accessed | tf_op | source)
XLA Modules:
  0.0 17.9 jit_solution(7135974058562332142)
XLA Ops:
  0.0 17.3 %shard_map.82 = bf16[1,32,128]{2,1,0:T(8,128)(2,1)S(1)} custom-call(bf16[4,8,128]{2,1,0:T(8,128)(2,1)} %q_hbm.1, bf16[2,2048,128]{2,1,0:T(8,128)(2,1)} %k_hbm.1, bf16[2,2048,128]{2,1,0:T(8,128)(2,1)} %v_hbm.1, bf16[1,2,128]{2,1,0:T(2,128)(2,1)} %bitcast.10, bf16[1,2,128]{2,1,0:T(2,128)(2,1)} %bitcast.11, s32[8]{0:T(128)} %owner_hbm.1, ...), custom_call_target="tpu_custom_call" | custom-call | tf_op jit(solution)/shard_map/pallas_call | solution.py:318
  17.3 0.6 %copy.10 = bf16[1,32,128]{2,1,0:T(8,128)(2,1)} copy(bf16[1,32,128]{2,1,0:T(8,128)(2,1)S(1)} %shard_map.82) | data formatting | bytes 16384

commit v5 on v2

--- a/solution.py
+++ b/solution.py
@@ -51,9 +51,7 @@
     fine_ref,
     q_all,
     part_values,
-    part_stats,
     landed_values,
-    landed_stats,
     in_sems,
     kv_sems,
     q_send,
@@ -155,7 +153,6 @@
     sub = lax.broadcasted_iota(jnp.int32, (pairs, heads, head_dim), 1)
     lane = lax.broadcasted_iota(jnp.int32, (pairs, heads, head_dim), 2)
     top = sub < per_group
-    diagonal = sub == lane
 
     def selection(first, g):
         chunk = lax.div(first, CHUNK)
@@ -203,17 +200,20 @@
         raw = q_all[pl.ds(first, width)].astype(jnp.float32).reshape(pairs, 2, heads, head_dim)
         queries = [one.reshape(rows, head_dim) for one in regroup(raw[:, 0], raw[:, 1])]
         (value_a, stat_a), (value_b, stat_b) = [attend(queries[g], g, *chosen[g]) for g in range(groups)]
-        values = [one.astype(jnp.bfloat16) for one in regroup(value_a, value_b)]
-        stats = [
-            jnp.sum(jnp.where(diagonal, one, 0.0), axis=1, keepdims=True) for one in regroup(stat_a, stat_b)
-        ]
+        values = regroup(value_a, value_b)
+        stats = regroup(stat_a, stat_b)
         for which in range(2):
+            stat = stats[which]
+            high = stat.astype(jnp.bfloat16).astype(jnp.float32)
+            middle = (stat - high).astype(jnp.bfloat16).astype(jnp.float32)
+            last = stat - high - middle
+            split = jnp.where(lane == 0, high, jnp.where(lane == 1, middle, jnp.where(lane == 2, last, 0.0)))
+            message = jnp.concatenate([values[which], split], axis=1).astype(jnp.bfloat16)
             for pair in range(pairs):
-                part_values[first + 2 * pair + which] = values[which][pair]
-                part_stats[first + 2 * pair + which] = stats[which][pair]
+                part_values[first + 2 * pair + which] = message[pair]
 
     slot = pl.ds(my_rep * seq_size + my_seq, 1)
-    messages = ((part_values, landed_values), (part_stats, landed_stats))
+    messages = ((part_values, landed_values),)
 
     def send_parts(first, start, skip):
         targets = width // out_rows
@@ -255,7 +255,6 @@
     send_parts(block_first(0), mine_at, 1)
     own = block_first(0) + mine_at * out_rows
     landed_values[slot] = part_values[pl.ds(own, out_rows)][None]
-    landed_stats[slot] = part_stats[pl.ds(own, out_rows)][None]
 
     if ahead:
         for away in range(1, near):
@@ -272,21 +271,18 @@
         got = landed.at[pl.ds(0, devices - 1)]
         pltpu.make_async_copy(got, got, p_recv.at[kind]).wait()
 
-    same = lax.broadcasted_iota(jnp.int32, (heads, head_dim), 0) == lax.broadcasted_iota(
-        jnp.int32, (heads, head_dim), 1
-    )
     for i in range(out_rows):
         for p in range(rep_size):
-            stats = [landed_stats[p * seq_size + s, i] for s in range(seq_size)]
+            stats, values = [], []
+            for s in range(seq_size):
+                message = landed_values[p * seq_size + s, i].astype(jnp.float32)
+                values.append(message[:heads])
+                stats.append(jnp.sum(message[heads:], axis=1, keepdims=True))
             peak = functools.reduce(jnp.maximum, stats)
             factors = [jnp.exp2(stat - peak) for stat in stats]
             total = functools.reduce(jnp.add, factors)
-            summed = jnp.zeros((heads, head_dim), jnp.float32)
-            for s in range(seq_size):
-                share = jnp.where(same, factors[s] / total, 0.0)
-                share = jnp.sum(share, axis=1, keepdims=True)
-                summed = summed + share * landed_values[p * seq_size + s, i].astype(jnp.float32)
-            out_ref[i, p * heads : (p + 1) * heads] = summed.astype(out_ref.dtype)
+            summed = functools.reduce(jnp.add, [f * v for f, v in zip(factors, values)])
+            out_ref[i, p * heads : (p + 1) * heads] = (summed / total).astype(out_ref.dtype)
 
     sent = q_all.at[pl.ds(0, (seq_size - 1) * own_rows)]
     pltpu.make_async_copy(sent, sent, q_send).wait()
@@ -329,10 +325,8 @@
                 pltpu.VMEM(super_ids.shape, super_ids.dtype),
                 pltpu.VMEM(fine_ids.shape, fine_ids.dtype),
                 pltpu.VMEM((seq_size * own_rows, heads, head_dim), jnp.bfloat16),
-                pltpu.VMEM((requests, heads, head_dim), jnp.bfloat16),
-                pltpu.VMEM((requests, 1, head_dim), jnp.float32),
-                pltpu.VMEM((devices, out_rows, heads, head_dim), jnp.bfloat16),
-                pltpu.VMEM((devices, out_rows, 1, head_dim), jnp.float32),
+                pltpu.VMEM((requests, 2 * heads, head_dim), jnp.bfloat16),
+                pltpu.VMEM((devices, out_rows, 2 * heads, head_dim), jnp.bfloat16),
                 pltpu.SemaphoreType.DMA((6,)),
                 pltpu.SemaphoreType.DMA((2, groups)),
                 pltpu.SemaphoreType.DMA,

time: 17.7 us -> 17.6 us (level)
  no operation moved by 1% of the time
where the time goes in v5:
time: 17.6 us; the launch traced here: 17.5 us
  Pallas kernels  16.9 us (96%)
  local copies, waits for them, and re-layouts  0.6 us (3%)
    pallas_call x1, Pallas kernels, shards(): pl.pallas_call(functools.partial(kernel, seq_size, rep_size), out_shape=p...  16.9 us
    unnamed x1, local copies, waits for them, and re-layouts  0.6 us

profile of v5, /device:TPU:0, one launch (start us, length us, event | category | flops | bytes accessed | tf_op | source)
XLA Modules:
  0.0 17.5 jit_solution(10468579249718469985)
XLA Ops:
  0.0 16.9 %shard_map.82 = bf16[1,32,128]{2,1,0:T(8,128)(2,1)S(1)} custom-call(bf16[4,8,128]{2,1,0:T(8,128)(2,1)} %q_hbm.1, bf16[2,2048,128]{2,1,0:T(8,128)(2,1)} %k_hbm.1, bf16[2,2048,128]{2,1,0:T(8,128)(2,1)} %v_hbm.1, bf16[1,2,128]{2,1,0:T(2,128)(2,1)} %bitcast.10, bf16[1,2,128]{2,1,0:T(2,128)(2,1)} %bitcast.11, s32[8]{0:T(128)} %owner_hbm.1, ...), custom_call_target="tpu_custom_call" | custom-call | tf_op jit(solution)/shard_map/pallas_call | solution.py:314
  16.9 0.6 %copy.10 = bf16[1,32,128]{2,1,0:T(8,128)(2,1)} copy(bf16[1,32,128]{2,1,0:T(8,128)(2,1)S(1)} %shard_map.82) | data formatting | bytes 16384
